TPU v7x, 128 devices: a whole 4x4x4 slice. The times are simulated.
128 devices in a mesh: seq: 32 (over y, z_lo, x), tp: 4 (over z_hi, core).
Axes of the slice: x: 4, y: 4, z: 4 (z_hi: 2, z_lo: 2; z = z_hi * 2 + z_lo), core: 2. Of those that a mesh axis runs over, the one named last changes fastest.
Arguments:
- tokens: bfloat16 [16384, 3584], P('seq'), may hold values from -6 to 6
- norm_gain: float32 [3584], replicated, may hold values from 0.5 to 1.5
- q_weight: bfloat16 [3584, 3584], P(None, 'tp'), may hold values from -0.09375 to 0.09375
- q_bias: float32 [3584], P('tp'), may hold values from -9 to 9
- k_weight: bfloat16 [3584, 512], P(None, 'tp'), may hold values from -0.09375 to 0.09375
- k_bias: float32 [512], P('tp'), may hold values from -9 to 9
- v_weight: bfloat16 [3584, 512], P(None, 'tp'), may hold values from -0.09375 to 0.09375
- v_bias: float32 [512], P('tp'), may hold values from -5 to 5
- o_weight: bfloat16 [3584, 3584], P('tp'), may hold values from -0.09375 to 0.09375
- doc_ids: int32 [16384], replicated, may hold values from 0 to 7, never falling along the last dimension, each value on 1 to 8704 neighbouring positions
Outputs:
- attn_out: bfloat16 [16384, 3584], P('seq', 'tp')
Inputs may be any that keep to these rules, and one draw needn't show every extreme that they name: `doc_ids`: document numbers never fall along the sequence; each document holds 1 to 8704 tokens and one holds exactly that many.
All inputs are finite; a program needn't handle non-finite values.
Results may differ from a plain program's by a relative error of at most 0.012.
Values may be sent and summed in bfloat16 or wider, within the bound.
A program may use at most 128 MiB of HBM per device.

v0:
```python
import functools

import jax
import jax.numpy as jnp
import numpy as np
from jax import lax
from jax.experimental import pallas as pl
from jax.experimental.pallas import tpu as pltpu
from jax.sharding import PartitionSpec as P

HD = 128
ROPE_BASE = 1000000.0
EPS = 1e-06
SCORE = float(np.log2(np.e) / np.sqrt(HD))
LOW = -1e30
Y, Z, X = 4, 2, 4
MESH = pl.DeviceIdType.MESH

SLOTS = [(0, 0, 0), (1, 0, 0), (0, 1, 0), (3, 0, 0), (0, 0, 1), (1, 0, 1), (1, 0, 3), (2, 0, 0),
 (1, 1, 1), (3, 1, 1), (1, 0, 2), (2, 0, 1), (3, 0, 3), (0, 1, 3), (0, 0, 2), (1, 1, 0),
 (2, 0, 2), (2, 0, 3), (2, 1, 0), (1, 1, 3), (2, 1, 1), (0, 1, 2), (2, 1, 2), (0, 0, 3),
 (2, 1, 3), (1, 1, 2), (0, 1, 1)]
MASKS = [0, 16777215, 252645135, 61166, 2139062271, 16777215, 16777215, 65535, 16777215, 128, 16777215,
 65535, 61166, 252645135, 858993459, 16777215, 64764, 61166, 61680, 16777215, 63736, 252645135,
 61680, 286331153, 61680, 16777215, 252645263]
POINTS = {2: [(1, 'x+', 5), (1, 'x-', 6), (1, 'y+', 7)],
 3: [(3, 'x-', 12)],
 4: [(2, 'x-', 13)],
 6: [(5, 'x+', 10)],
 7: [(5, 'z', 8)],
 8: [(4, 'x+', 14)],
 9: [(6, 'z', 19)],
 10: [(5, 'y+', 11)],
 11: [(4, 'z', 26)],
 13: [(7, 'z', 18)],
 16: [(8, 'x-', 15), (8, 'x+', 25)],
 17: [(10, 'y+', 16), (12, 'y-', 17)],
 21: [(13, 'x-', 21)],
 22: [(8, 'y+', 20)],
 24: [(16, 'z', 22)],
 28: [(18, 'x-', 24)],
 50: [(26, 'y-', 9)]}
FIRST = [(0, 'y+', 1), (0, 'z', 2), (0, 'y-', 3), (0, 'x+', 4), (0, 'x-', 23)]
ZCHUNKS = 4
PARTS = 2
SUBS = 4
TOKEN_LOADS = 4
RELAY_STEPS = (3, 5, 6, 7)
DEFER = 15


def kernel(
    tok_hbm, gain_ref, wq_hbm, wk_hbm, wv_hbm, wo_hbm, qb_ref, kb_ref, vb_ref, doc_ref,
    cosr_ref, sinr_ref, cosb_ref, sinb_ref, out_ref,
    tok, normed, wq, wkv, wo, kbuf, vbuf, qa, acc, top, sbuf, pbuf, fade, ctx,
    term, pair_in, zsend, relay, zin,
    load_sem, send_sem, recv_sem, pair_send, pair_recv, z_send, z_recv, hop_send, hop_recv,
):
    rows, width = tok.shape
    heads = qb_ref.shape[0]
    cols = out_ref.shape[1]
    lanes = rows // HD
    me = lax.axis_index("seq")
    tp = lax.axis_index("tp")
    y, z, x = me // (Z * X), me // X % Z, me % X
    zhi, core = tp // 2, tp % 2

    token_rows = rows // TOKEN_LOADS
    token_loads = [
        pltpu.make_async_copy(
            tok_hbm.at[pl.ds(i * token_rows, token_rows), :],
            tok.at[pl.ds(i * token_rows, token_rows), :],
            load_sem.at[4 + i],
        )
        for i in range(TOKEN_LOADS)
    ]
    load_k = pltpu.make_async_copy(wk_hbm, wkv.at[:, 0:HD], load_sem.at[0])
    load_v = pltpu.make_async_copy(wv_hbm, wkv.at[:, HD : 2 * HD], load_sem.at[1])
    load_q = pltpu.make_async_copy(wq_hbm, wq, load_sem.at[2])
    load_o = pltpu.make_async_copy(wo_hbm, wo, load_sem.at[3])
    for load in token_loads:
        load.start()
    load_k.start()
    load_v.start()

    def at(yy, zz, xx):
        return (yy * Z + zz) * X + xx

    level = zhi * Z + z
    up, down = (level + 1) % (2 * Z), (level + 2 * Z - 1) % (2 * Z)
    z_up = (at(y, up % Z, x), up // Z * 2 + core)
    z_down = (at(y, down % Z, x), down // Z * 2 + core)
    mate = (me, zhi * 2 + 1 - core)
    seq_to = {
        "y+": (at((y + 1) % Y, z, x), tp),
        "y-": (at((y + Y - 1) % Y, z, x), tp),
        "x+": (at(y, z, (x + 1) % X), tp),
        "x-": (at(y, z, (x + X - 1) % X), tp),
        "z": (at(y, (z + 1) % Z, x), tp),
    }
    barrier = pltpu.get_barrier_semaphore()
    greeted = [seq_to[d] for d in ("y+", "y-", "x+", "x-")] + [z_up, z_down, mate]
    for device in greeted:
        pl.semaphore_signal(barrier, inc=1, device_id=device, device_id_type=MESH)

    def source(slot):
        oy, oz, ox = SLOTS[slot]
        return at((y + Y - oy) % Y, (z + oz) % Z, (x + X - ox) % X)

    def goes(mask, maker):
        value = mask - (1 << 32) if mask >= 1 << 31 else mask
        return lax.shift_right_logical(jnp.int32(value), maker) % 2 != 0

    def documents(block):
        return jnp.concatenate(
            [doc_ref[pl.ds(block * lanes + i, 1), :] for i in range(lanes)], axis=1
        )

    number = lax.broadcasted_iota(jnp.int32, (HD, rows), 0)
    for slot in range(len(SLOTS)):
        docs = documents(source(slot))
        kbuf[slot, HD : 2 * HD, :] = (number == docs).astype(jnp.float32).astype(jnp.bfloat16)
        vbuf[slot, :, HD : 2 * HD] = jnp.ones((rows, HD), jnp.bfloat16)
    part_rows = rows // PARTS
    other = jnp.where(number == documents(me), 0.0, LOW).T.astype(jnp.bfloat16)
    for part in range(PARTS):
        for head in range(heads):
            first = (part * heads + head) * part_rows
            qa[first : first + part_rows, HD : 2 * HD] = other[
                part * part_rows : (part + 1) * part_rows, :
            ]

    gain = jnp.concatenate([gain_ref[i : i + 1, :] for i in range(width // HD)], axis=1)
    piece = min(32, token_rows)

    def norm_rows(index, carry):
        span = pl.ds(pl.multiple_of(index * piece, piece), piece)
        wide = tok[span, :].astype(jnp.float32)
        scale = lax.rsqrt(jnp.sum(wide * wide, axis=1, keepdims=True) * (1.0 / width) + EPS)
        normed[span, :] = (wide * scale * gain).astype(jnp.bfloat16)
        return carry

    per = token_rows // piece
    for i in range(TOKEN_LOADS):
        token_loads[i].wait()
        if i == TOKEN_LOADS - 1:
            load_k.wait()
            load_v.wait()
            load_q.start()
        lax.fori_loop(i * per, (i + 1) * per, norm_rows, 0)
    load_o.start()

    cosb = cosb_ref[pl.ds(me, 1), :]
    sinb = sinb_ref[pl.ds(me, 1), :]

    def rotate(t):
        lane = lax.broadcasted_iota(jnp.int32, (1, HD), 1)
        sign = jnp.where(lane < HD // 2, -1.0, 1.0)
        cosr, sinr = cosr_ref[...], sinr_ref[...]
        cos = cosr * cosb - sinr * sinb
        sin = (sinr * cosb + cosr * sinb) * sign
        return t * cos + pltpu.roll(t, HD // 2, 1) * sin

    kv = jnp.dot(normed[...], wkv[...], preferred_element_type=jnp.float32)
    keys = rotate(kv[:, 0:HD] + kb_ref[...])
    kbuf[0, 0:HD, :] = keys.T.astype(jnp.bfloat16)
    vbuf[0, :, 0:HD] = (kv[:, HD : 2 * HD] + vb_ref[...]).astype(jnp.bfloat16)

    def edge(half, origin, direction, landing):
        ref = (lambda s: kbuf.at[s, 0:HD, :]) if half == 0 else (lambda s: vbuf.at[s, :, 0:HD])
        return pltpu.make_async_remote_copy(
            src_ref=ref(origin),
            dst_ref=ref(landing),
            send_sem=send_sem.at[landing, half],
            recv_sem=recv_sem.at[landing, half],
            device_id=seq_to[direction],
            device_id_type=MESH,
        )

    def arrived(half, slot):
        edge(half, slot, "y+", slot).wait_recv()

    pl.semaphore_wait(barrier, len(greeted))

    for half in range(2):
        for origin, direction, landing in FIRST:
            @pl.when(goes(MASKS[landing], me))
            def _():
                edge(half, origin, direction, landing).start()

    load_q.wait()

    def project(first, count):
        both = jnp.dot(
            normed[...], wq[:, pl.ds(first, count * HD)], preferred_element_type=jnp.float32
        )
        for i in range(count):
            head = first // HD + i
            turned = rotate(both[:, i * HD : (i + 1) * HD] + qb_ref[pl.ds(head, 1), :])
            for part in range(PARTS):
                start = pl.multiple_of((part * heads + head) * part_rows, part_rows)
                qa[pl.ds(start, part_rows), 0:HD] = turned[
                    part * part_rows : (part + 1) * part_rows, :
                ].astype(jnp.bfloat16)

    def project_pair(index, carry):
        project(pl.multiple_of(index * 2 * HD, 2 * HD), 2)
        return carry

    lax.fori_loop(0, heads // 2, project_pair, 0)
    if heads % 2:
        project((heads - 1) * HD, 1)

    sub = heads * part_rows // SUBS

    def attend(slot, part, own):
        count = (part + 1) * part_rows if own else rows

        def scores(index):
            first = part * heads * part_rows + index * sub
            sbuf[index % 2, :, 0:count] = jnp.dot(
                qa[first : first + sub, :], kbuf[slot, :, 0:count], preferred_element_type=jnp.float32
            )

        def weigh(index):
            first = part * heads * part_rows + index * sub
            span = slice(first, first + sub)
            s = sbuf[index % 2, :, 0:count] * SCORE
            if own:
                qpos = lax.broadcasted_iota(jnp.int32, (sub, count), 0) + index * sub
                qpos = qpos % part_rows + part * part_rows
                kpos = lax.broadcasted_iota(jnp.int32, (sub, count), 1)
                s = jnp.where(kpos <= qpos, s, LOW)
                fresh = jnp.broadcast_to(jnp.max(s, axis=1, keepdims=True), (sub, HD))
            else:
                before = top[span, :]
                fresh = jnp.maximum(before, jnp.max(s, axis=1, keepdims=True))
                fade[index % 2] = jnp.exp2(before - fresh)
            top[span, :] = fresh
            pbuf[index % 2, :, 0:count] = jnp.exp2(s - jnp.tile(fresh, (1, count // HD))).astype(
                jnp.bfloat16
            )

        def gather(index):
            first = part * heads * part_rows + index * sub
            span = slice(first, first + sub)
            added = jnp.dot(
                pbuf[index % 2, :, 0:count], vbuf[slot, 0:count, :], preferred_element_type=jnp.float32
            )
            if own:
                acc[span, :] = added
            else:
                acc[span, :] = acc[span, :] * jnp.tile(fade[index % 2], (1, 2)) + added

        for step in range(SUBS + 2):
            if step < SUBS:
                scores(step)
            if 0 <= step - 2:
                gather(step - 2)
            if 0 <= step - 1 < SUBS:
                weigh(step - 1)

    away, home = 1 - zhi, zhi
    chunk = part_rows // (2 * ZCHUNKS)

    def span_of(way, index):
        return pl.ds((way * ZCHUNKS + index) * chunk, chunk)

    def to_mate(part, index):
        return pltpu.make_async_remote_copy(
            src_ref=term.at[part, index],
            dst_ref=pair_in.at[part, index],
            send_sem=pair_send.at[part, index],
            recv_sem=pair_recv.at[part, index],
            device_id=mate,
            device_id_type=MESH,
        )

    def first_hop(part, way, index):
        return pltpu.make_async_remote_copy(
            src_ref=zsend.at[part, span_of(way, index), :],
            dst_ref=relay.at[part, span_of(way, index), :],
            send_sem=hop_send.at[part, way, index],
            recv_sem=hop_recv.at[part, way, index],
            device_id=(z_up, z_down)[way],
            device_id_type=MESH,
        )

    def second_hop(part, way, index):
        return pltpu.make_async_remote_copy(
            src_ref=relay.at[part, span_of(way, index), :],
            dst_ref=zin.at[part, span_of(way, index), :],
            send_sem=z_send.at[part, way, index],
            recv_sem=z_recv.at[part, way, index],
            device_id=(z_up, z_down)[way],
            device_id_type=MESH,
        )

    def finish_heads(part):
        for head in range(heads):
            first = (part * heads + head) * part_rows
            span = slice(first, first + part_rows)
            ctx[part * part_rows : (part + 1) * part_rows, head * HD : (head + 1) * HD] = (
                acc[span, 0:HD] / acc[span, HD : 2 * HD]
            ).astype(jnp.bfloat16)

    def product(part, block):
        return jnp.dot(
            ctx[part * part_rows : (part + 1) * part_rows, :],
            wo[:, pl.ds(pl.multiple_of(block * cols, HD), cols)],
            preferred_element_type=jnp.float32,
        ).astype(jnp.bfloat16)

    def give(part):
        finish_heads(part)
        term[part, 0] = product(part, away * 2 + 1 - core)
        zsend[part] = product(part, away * 2 + core)
        to_mate(part, 0).start()
        term[part, 1] = product(part, home * 2 + 1 - core)
        to_mate(part, 1).start()

    def pass_first(part):
        to_mate(part, 0).wait_recv()
        for index in range(ZCHUNKS):
            for way in range(2):
                span = span_of(way, index)
                zsend[part, span, :] = (
                    zsend[part, span, :].astype(jnp.float32)
                    + pair_in[part, 0, span, :].astype(jnp.float32)
                ).astype(jnp.bfloat16)
            if index > 0:
                for way in range(2):
                    first_hop(part, way, index - 1).start()
        for way in range(2):
            first_hop(part, way, ZCHUNKS - 1).start()

    def keep(part):
        out_ref[part * part_rows : (part + 1) * part_rows, :] = product(part, home * 2 + core)

    def pass_second(part, index):
        for way in range(2):
            first_hop(part, way, index).wait_recv()
            second_hop(part, way, index).start()

    def take(part):
        to_mate(part, 1).wait_recv()
        for index in range(ZCHUNKS):
            for way in range(2):
                second_hop(part, way, index).wait_recv()
                span = span_of(way, index)
                target = pl.ds(part * part_rows + (way * ZCHUNKS + index) * chunk, chunk)
                out_ref[target, :] = (
                    out_ref[target, :].astype(jnp.float32)
                    + pair_in[part, 1, span, :].astype(jnp.float32)
                    + zin[part, span, :].astype(jnp.float32)
                ).astype(jnp.bfloat16)

    attend(0, 0, True)
    attend(0, 1, True)

    kids = {}
    for edges in POINTS.values():
        for origin, direction, landing in edges:
            kids.setdefault(origin, []).append(landing)
    sent_on = {slot: 0 for slot in range(len(SLOTS))}
    for origin, landings in kids.items():
        for landing in landings:
            sent_on[origin] |= MASKS[landing]

    wanted = jnp.int32(0)
    late = jnp.int32(0)
    for slot in range(len(SLOTS) - 1, 0, -1):
        maker = source(slot)
        back = me - maker
        near = (back > 0) & (back <= (Y * Z * X) // 2 + 1)
        wanted = wanted * 2 + near.astype(jnp.int32)
        late = late * 2 + goes(MASKS[slot] & ~sent_on[slot], maker).astype(jnp.int32)

    planned = {}
    awaited = set()
    for when in sorted(POINTS):
        fresh = [o for o in dict.fromkeys(e[0] for e in POINTS[when]) if o not in awaited]
        awaited |= set(fresh)
        planned[when] = fresh

    def send_on(when):
        for half in range(2):
            seen = set()
            for origin, direction, landing in POINTS[when]:
                maker = source(origin)
                if origin in planned[when] and origin not in seen:
                    seen.add(origin)

                    @pl.when(goes(sent_on[origin], maker))
                    def _():
                        arrived(half, origin)

                @pl.when(goes(MASKS[landing], maker))
                def _():
                    edge(half, origin, direction, landing).start()

    def visit(step, carry):
        left, unseen = carry
        for when in sorted(POINTS):
            if when % 2 == 0:
                pl.when(step == when // 2)(functools.partial(send_on, when))

        @pl.when(unseen % 2 == 1)
        def _():
            arrived(0, step)
            arrived(1, step)

        @pl.when(left % 2 == 1)
        def _():
            attend(step, 0, False)

        for when in sorted(POINTS):
            if when % 2 == 1:
                pl.when(step == when // 2)(functools.partial(send_on, when))

        @pl.when((left % 2 == 1) & (step < DEFER))
        def _():
            attend(step, 1, False)

        return left // 2, unseen // 2

    lax.fori_loop(1, len(SLOTS), visit, (wanted, late))

    load_o.wait()
    give(0)
    for slot in range(1, DEFER):
        wanted = wanted // 2

    def again(step, left):
        @pl.when(step == DEFER + 1)
        def _():
            pass_first(0)

        for index in range(ZCHUNKS):
            @pl.when(step == DEFER + RELAY_STEPS[index])
            def _():
                pass_second(0, index)

        @pl.when(left % 2 == 1)
        def _():
            attend(step, 1, False)

        return left // 2

    lax.fori_loop(DEFER, len(SLOTS), again, wanted)
    for index in range(ZCHUNKS):
        if DEFER + RELAY_STEPS[index] >= len(SLOTS):
            pass_second(0, index)
    keep(0)

    last = PARTS - 1
    give(last)
    pass_first(last)
    keep(last)
    take(0)
    for index in range(ZCHUNKS):
        pass_second(last, index)
    take(last)

    for origin, direction, landing in FIRST:
        @pl.when(goes(MASKS[landing], me))
        def _():
            for half in range(2):
                edge(half, origin, direction, landing).wait_send()

    for edges in POINTS.values():
        for origin, direction, landing in edges:
            @pl.when(goes(MASKS[landing], source(origin)))
            def _():
                for half in range(2):
                    edge(half, origin, direction, landing).wait_send()

    for part in range(PARTS):
        for index in range(2):
            to_mate(part, index).wait_send()
        for index in range(ZCHUNKS):
            for way in range(2):
                first_hop(part, way, index).wait_send()
                second_hop(part, way, index).wait_send()


def body(
    tokens, norm_gain, q_weight, q_bias, k_weight, k_bias, v_weight, v_bias, o_weight, doc_ids
):
    rows, width = tokens.shape
    blocks = doc_ids.shape[0] // rows
    heads = q_weight.shape[1] // HD
    cols = o_weight.shape[1] // lax.axis_size("tp")
    freq = ROPE_BASE ** (-2.0 * np.arange(HD // 2) / HD)
    freq = np.concatenate([freq, freq])
    inner = np.arange(rows)[:, None] * freq
    outer = (np.arange(blocks) * rows)[:, None] * freq
    f32, bf16 = jnp.float32, jnp.bfloat16
    vmem = pl.BlockSpec(memory_space=pltpu.VMEM)
    hbm = pl.BlockSpec(memory_space=pl.ANY)
    dma = pltpu.SemaphoreType.DMA
    return pl.pallas_call(
        kernel,
        out_shape=jax.ShapeDtypeStruct((rows, cols), bf16),
        in_specs=[hbm, vmem, hbm, hbm, hbm, hbm] + [vmem] * 8,
        out_specs=vmem,
        scratch_shapes=[
            pltpu.VMEM((rows, width), bf16),
            pltpu.VMEM((rows, width), bf16),
            pltpu.VMEM(q_weight.shape, bf16),
            pltpu.VMEM((width, 2 * HD), bf16),
            pltpu.VMEM(o_weight.shape, bf16),
            pltpu.VMEM((len(SLOTS), 2 * HD, rows), bf16),
            pltpu.VMEM((len(SLOTS), rows, 2 * HD), bf16),
            pltpu.VMEM((heads * rows, 2 * HD), bf16),
            pltpu.VMEM((heads * rows, 2 * HD), f32),
            pltpu.VMEM((heads * rows, HD), f32),
            pltpu.VMEM((2, heads * rows // PARTS // SUBS, rows), f32),
            pltpu.VMEM((2, heads * rows // PARTS // SUBS, rows), bf16),
            pltpu.VMEM((2, heads * rows // PARTS // SUBS, HD), f32),
            pltpu.VMEM((rows, heads * HD), bf16),
            pltpu.VMEM((PARTS, 2, rows // PARTS, cols), bf16),
            pltpu.VMEM((PARTS, 2, rows // PARTS, cols), bf16),
            pltpu.VMEM((PARTS, rows // PARTS, cols), bf16),
            pltpu.VMEM((PARTS, rows // PARTS, cols), bf16),
            pltpu.VMEM((PARTS, rows // PARTS, cols), bf16),
            dma((TOKEN_LOADS + 4,)),
            dma((len(SLOTS), 2)),
            dma((len(SLOTS), 2)),
            dma((PARTS, 2)),
            dma((PARTS, 2)),
            dma((PARTS, 2, ZCHUNKS)),
            dma((PARTS, 2, ZCHUNKS)),
            dma((PARTS, 2, ZCHUNKS)),
            dma((PARTS, 2, ZCHUNKS)),
        ],
        compiler_params=pltpu.CompilerParams(
            collective_id=0, has_side_effects=True, vmem_limit_bytes=67043328
        ),
    )(
        tokens,
        norm_gain.reshape(-1, HD),
        q_weight,
        k_weight,
        v_weight,
        o_weight,
        q_bias.reshape(-1, HD),
        k_bias.reshape(1, -1),
        v_bias.reshape(1, -1),
        doc_ids.reshape(-1, HD),
        jnp.asarray(np.cos(inner), f32),
        jnp.asarray(np.sin(inner), f32),
        jnp.asarray(np.cos(outer), f32),
        jnp.asarray(np.sin(outer), f32),
    )


def solution(mesh):
    placed = (
        P("seq", None),
        P(),
        P(None, "tp"),
        P("tp"),
        P(None, "tp"),
        P("tp"),
        P(None, "tp"),
        P("tp"),
        P("tp", None),
        P(),
    )
    return jax.shard_map(
        body, mesh=mesh, in_specs=placed, out_specs=P("seq", "tp"), check_vma=False
    )
```

profile of v0, /device:TPU:55, one launch (start us, length us, event | category | flops | bytes accessed | tf_op | source)
XLA Modules:
  0.0 105.1 jit_solution(6648468447772660740)
XLA Ops:
  0.0 102.9 %shard_map.136 = bf16[512,896]{1,0:T(8,128)(2,1)} custom-call(bf16[512,3584]{1,0:T(8,128)(2,1)} %tok_hbm.1, f32[28,128]{1,0:T(8,128)} %bitcast.6, bf16[3584,896]{1,0:T(8,128)(2,1)} %wq_hbm.1, bf16[3584,128]{1,0:T(8,128)(2,1)} %wk_hbm.1, bf16[3584,128]{1,0:T(8,128)(2,1)} %wv_hbm.1, bf16[896,3584]{1,0:T(8,128)(2,1)} %wo_hbm.1, f32[7,128]{1,0:T(8,128)} %bitcast.7, ...), custom_call_target="tpu_custom_call" | custom-call | tf_op jit(solution)/shard_map/pallas_call | solution.py:502
  102.9 2.2 %copy.16 = bf16[512,896]{1,0:T(8,128)(2,1)} copy(bf16[512,896]{1,0:T(8,128)(2,1)} %shard_map.136) | data formatting | bytes 1835008
where the time goes:
time: 105 us
  Pallas kernels  103 us (98%)
  local copies, waits for them, and re-layouts  2.18 us (2%)
    pallas_call x1, Pallas kernels, body(): pl.pallas_call(kernel, out_shape=jax.ShapeDtypeStruct((rows, cols), bf16)...  103 us
    unnamed x1, local copies, waits for them, and re-layouts  2.18 us

commit v1 on v0

--- a/solution.py
+++ b/solution.py
@@ -16,37 +16,34 @@
 Y, Z, X = 4, 2, 4
 MESH = pl.DeviceIdType.MESH
 
-SLOTS = [(0, 0, 0), (1, 0, 0), (0, 1, 0), (3, 0, 0), (0, 0, 1), (1, 0, 1), (1, 0, 3), (2, 0, 0),
- (1, 1, 1), (3, 1, 1), (1, 0, 2), (2, 0, 1), (3, 0, 3), (0, 1, 3), (0, 0, 2), (1, 1, 0),
- (2, 0, 2), (2, 0, 3), (2, 1, 0), (1, 1, 3), (2, 1, 1), (0, 1, 2), (2, 1, 2), (0, 0, 3),
- (2, 1, 3), (1, 1, 2), (0, 1, 1)]
-MASKS = [0, 16777215, 252645135, 61166, 2139062271, 16777215, 16777215, 65535, 16777215, 128, 16777215,
- 65535, 61166, 252645135, 858993459, 16777215, 64764, 61166, 61680, 16777215, 63736, 252645135,
- 61680, 286331153, 61680, 16777215, 252645263]
-POINTS = {2: [(1, 'x+', 5), (1, 'x-', 6), (1, 'y+', 7)],
- 3: [(3, 'x-', 12)],
- 4: [(2, 'x-', 13)],
- 6: [(5, 'x+', 10)],
- 7: [(5, 'z', 8)],
- 8: [(4, 'x+', 14)],
- 9: [(6, 'z', 19)],
- 10: [(5, 'y+', 11)],
- 11: [(4, 'z', 26)],
- 13: [(7, 'z', 18)],
- 16: [(8, 'x-', 15), (8, 'x+', 25)],
- 17: [(10, 'y+', 16), (12, 'y-', 17)],
- 21: [(13, 'x-', 21)],
- 22: [(8, 'y+', 20)],
- 24: [(16, 'z', 22)],
- 28: [(18, 'x-', 24)],
- 50: [(26, 'y-', 9)]}
-FIRST = [(0, 'y+', 1), (0, 'z', 2), (0, 'y-', 3), (0, 'x+', 4), (0, 'x-', 23)]
+SLOTS = [(0, 0, 0), (1, 0, 0), (0, 1, 0), (0, 0, 1), (2, 0, 0), (1, 1, 0), (1, 0, 3), (3, 1, 1),
+ (1, 0, 1), (1, 1, 3), (0, 0, 3), (1, 0, 2), (0, 1, 3), (2, 1, 3), (0, 0, 2), (2, 1, 0),
+ (0, 1, 2), (2, 0, 3), (2, 0, 1), (2, 1, 2), (1, 1, 2), (1, 1, 1), (2, 1, 1), (2, 0, 2),
+ (0, 1, 1)]
+MASKS = [0, 16777215, 252645263, 2013265919, 65535, 16777215, 16777215, 128, 16777215, 16777215,
+ 286331153, 16777215, 252645135, 61680, 858993459, 63736, 252645135, 61166, 65535, 61680,
+ 16777215, 16777215, 63736, 52428, 252645263]
+POINTS = {2: [(1, 'y+', 4), (1, 'z', 5), (1, 'x-', 6), (2, 'x+', 24)],
+ 3: [(2, 'x-', 12)],
+ 4: [(3, 'y+', 8)],
+ 6: [(3, 'x+', 14)],
+ 8: [(4, 'z', 15), (6, 'y+', 17)],
+ 9: [(5, 'x-', 9)],
+ 12: [(4, 'x+', 18), (6, 'x-', 11)],
+ 15: [(9, 'y+', 13)],
+ 16: [(8, 'z', 21)],
+ 18: [(12, 'x-', 16)],
+ 19: [(15, 'x+', 22)],
+ 20: [(11, 'z', 20)],
+ 22: [(11, 'y+', 23), (13, 'x-', 19)],
+ 48: [(24, 'y-', 7)]}
+FIRST = [(0, 'y+', 1), (0, 'z', 2), (0, 'x+', 3), (0, 'x-', 10)]
 ZCHUNKS = 4
-PARTS = 2
-SUBS = 4
+SHARES = (2, 4, 4)
+PARTS = len(SHARES)
+SUBS = 8
 TOKEN_LOADS = 4
-RELAY_STEPS = (3, 5, 6, 7)
-DEFER = 15
+DEFER = 17
 
 
 def kernel(
@@ -121,14 +118,16 @@
         docs = documents(source(slot))
         kbuf[slot, HD : 2 * HD, :] = (number == docs).astype(jnp.float32).astype(jnp.bfloat16)
         vbuf[slot, :, HD : 2 * HD] = jnp.ones((rows, HD), jnp.bfloat16)
-    part_rows = rows // PARTS
+    part_rows = [rows // share for share in SHARES]
+    part_start = [sum(part_rows[:i]) for i in range(PARTS)]
+    sub = heads * rows // SUBS
+    sub_start = [heads * start // sub for start in part_start]
     other = jnp.where(number == documents(me), 0.0, LOW).T.astype(jnp.bfloat16)
     for part in range(PARTS):
         for head in range(heads):
-            first = (part * heads + head) * part_rows
-            qa[first : first + part_rows, HD : 2 * HD] = other[
-                part * part_rows : (part + 1) * part_rows, :
-            ]
+            count, begin = part_rows[part], part_start[part]
+            first = heads * begin + head * count
+            qa[first : first + count, HD : 2 * HD] = other[begin : begin + count, :]
 
     gain = jnp.concatenate([gain_ref[i : i + 1, :] for i in range(width // HD)], axis=1)
     piece = min(32, token_rows)
@@ -198,10 +197,9 @@
             head = first // HD + i
             turned = rotate(both[:, i * HD : (i + 1) * HD] + qb_ref[pl.ds(head, 1), :])
             for part in range(PARTS):
-                start = pl.multiple_of((part * heads + head) * part_rows, part_rows)
-                qa[pl.ds(start, part_rows), 0:HD] = turned[
-                    part * part_rows : (part + 1) * part_rows, :
-                ].astype(jnp.bfloat16)
+                size, begin = part_rows[part], part_start[part]
+                start = pl.multiple_of(heads * begin + head * size, size)
+                qa[pl.ds(start, size), 0:HD] = turned[begin : begin + size, :].astype(jnp.bfloat16)
 
     def project_pair(index, carry):
         project(pl.multiple_of(index * 2 * HD, 2 * HD), 2)
@@ -211,65 +209,65 @@
     if heads % 2:
         project((heads - 1) * HD, 1)
 
-    sub = heads * part_rows // SUBS
-
-    def attend(slot, part, own):
-        count = (part + 1) * part_rows if own else rows
-
-        def scores(index):
-            first = part * heads * part_rows + index * sub
-            sbuf[index % 2, :, 0:count] = jnp.dot(
-                qa[first : first + sub, :], kbuf[slot, :, 0:count], preferred_element_type=jnp.float32
+    def attend(slot, runs, own=0):
+        count = own or rows
+
+        def scores(turn, run):
+            sbuf[turn % 2, :, 0:count] = jnp.dot(
+                qa[run * sub : (run + 1) * sub, :],
+                kbuf[slot, :, 0:count],
+                preferred_element_type=jnp.float32,
             )
 
-        def weigh(index):
-            first = part * heads * part_rows + index * sub
-            span = slice(first, first + sub)
-            s = sbuf[index % 2, :, 0:count] * SCORE
+        def weigh(turn, run):
+            span = slice(run * sub, (run + 1) * sub)
+            s = sbuf[turn % 2, :, 0:count] * SCORE
             if own:
-                qpos = lax.broadcasted_iota(jnp.int32, (sub, count), 0) + index * sub
-                qpos = qpos % part_rows + part * part_rows
+                part = max(p for p in range(PARTS) if sub_start[p] <= run)
+                qpos = lax.broadcasted_iota(jnp.int32, (sub, count), 0)
+                qpos = (qpos + (run - sub_start[part]) * sub) % part_rows[part] + part_start[part]
                 kpos = lax.broadcasted_iota(jnp.int32, (sub, count), 1)
                 s = jnp.where(kpos <= qpos, s, LOW)
                 fresh = jnp.broadcast_to(jnp.max(s, axis=1, keepdims=True), (sub, HD))
             else:
                 before = top[span, :]
                 fresh = jnp.maximum(before, jnp.max(s, axis=1, keepdims=True))
-                fade[index % 2] = jnp.exp2(before - fresh)
+                fade[turn % 2] = jnp.exp2(before - fresh)
             top[span, :] = fresh
-            pbuf[index % 2, :, 0:count] = jnp.exp2(s - jnp.tile(fresh, (1, count // HD))).astype(
+            pbuf[turn % 2, :, 0:count] = jnp.exp2(s - jnp.tile(fresh, (1, count // HD))).astype(
                 jnp.bfloat16
             )
 
-        def gather(index):
-            first = part * heads * part_rows + index * sub
-            span = slice(first, first + sub)
+        def gather(turn, run):
+            span = slice(run * sub, (run + 1) * sub)
             added = jnp.dot(
-                pbuf[index % 2, :, 0:count], vbuf[slot, 0:count, :], preferred_element_type=jnp.float32
+                pbuf[turn % 2, :, 0:count], vbuf[slot, 0:count, :], preferred_element_type=jnp.float32
             )
             if own:
                 acc[span, :] = added
             else:
-                acc[span, :] = acc[span, :] * jnp.tile(fade[index % 2], (1, 2)) + added
-
-        for step in range(SUBS + 2):
-            if step < SUBS:
-                scores(step)
-            if 0 <= step - 2:
-                gather(step - 2)
-            if 0 <= step - 1 < SUBS:
-                weigh(step - 1)
+                acc[span, :] = acc[span, :] * jnp.tile(fade[turn % 2], (1, 2)) + added
+
+        for turn in range(len(runs) + 2):
+            if turn < len(runs):
+                scores(turn, runs[turn])
+            if 0 <= turn - 2:
+                gather(turn - 2, runs[turn - 2])
+            if 0 <= turn - 1 < len(runs):
+                weigh(turn - 1, runs[turn - 1])
 
     away, home = 1 - zhi, zhi
-    chunk = part_rows // (2 * ZCHUNKS)
-
-    def span_of(way, index):
-        return pl.ds((way * ZCHUNKS + index) * chunk, chunk)
+    chunk = rows // 16
+    chunks = [size // (2 * chunk) for size in part_rows]
+    part_span = [pl.ds(part_start[p], part_rows[p]) for p in range(PARTS)]
+
+    def span_of(part, way, index):
+        return pl.ds(part_start[part] + (way * chunks[part] + index) * chunk, chunk)
 
     def to_mate(part, index):
         return pltpu.make_async_remote_copy(
-            src_ref=term.at[part, index],
-            dst_ref=pair_in.at[part, index],
+            src_ref=term.at[index, part_span[part], :],
+            dst_ref=pair_in.at[index, part_span[part], :],
             send_sem=pair_send.at[part, index],
             recv_sem=pair_recv.at[part, index],
             device_id=mate,
@@ -278,8 +276,8 @@
 
     def first_hop(part, way, index):
         return pltpu.make_async_remote_copy(
-            src_ref=zsend.at[part, span_of(way, index), :],
-            dst_ref=relay.at[part, span_of(way, index), :],
+            src_ref=zsend.at[span_of(part, way, index), :],
+            dst_ref=relay.at[span_of(part, way, index), :],
             send_sem=hop_send.at[part, way, index],
             recv_sem=hop_recv.at[part, way, index],
             device_id=(z_up, z_down)[way],
@@ -288,8 +286,8 @@
 
     def second_hop(part, way, index):
         return pltpu.make_async_remote_copy(
-            src_ref=relay.at[part, span_of(way, index), :],
-            dst_ref=zin.at[part, span_of(way, index), :],
+            src_ref=relay.at[span_of(part, way, index), :],
+            dst_ref=zin.at[span_of(part, way, index), :],
             send_sem=z_send.at[part, way, index],
             recv_sem=z_recv.at[part, way, index],
             device_id=(z_up, z_down)[way],
@@ -297,45 +295,45 @@
         )
 
     def finish_heads(part):
+        size, begin = part_rows[part], part_start[part]
         for head in range(heads):
-            first = (part * heads + head) * part_rows
-            span = slice(first, first + part_rows)
-            ctx[part * part_rows : (part + 1) * part_rows, head * HD : (head + 1) * HD] = (
+            first = heads * begin + head * size
+            span = slice(first, first + size)
+            ctx[begin : begin + size, head * HD : (head + 1) * HD] = (
                 acc[span, 0:HD] / acc[span, HD : 2 * HD]
             ).astype(jnp.bfloat16)
 
     def product(part, block):
         return jnp.dot(
-            ctx[part * part_rows : (part + 1) * part_rows, :],
+            ctx[part_span[part], :],
             wo[:, pl.ds(pl.multiple_of(block * cols, HD), cols)],
             preferred_element_type=jnp.float32,
         ).astype(jnp.bfloat16)
 
     def give(part):
         finish_heads(part)
-        term[part, 0] = product(part, away * 2 + 1 - core)
-        zsend[part] = product(part, away * 2 + core)
+        term[0, part_span[part], :] = product(part, away * 2 + 1 - core)
+        zsend[part_span[part], :] = product(part, away * 2 + core)
         to_mate(part, 0).start()
-        term[part, 1] = product(part, home * 2 + 1 - core)
+        term[1, part_span[part], :] = product(part, home * 2 + 1 - core)
         to_mate(part, 1).start()
 
     def pass_first(part):
         to_mate(part, 0).wait_recv()
-        for index in range(ZCHUNKS):
+        for index in range(chunks[part]):
             for way in range(2):
-                span = span_of(way, index)
-                zsend[part, span, :] = (
-                    zsend[part, span, :].astype(jnp.float32)
-                    + pair_in[part, 0, span, :].astype(jnp.float32)
+                span = span_of(part, way, index)
+                zsend[span, :] = (
+                    zsend[span, :].astype(jnp.float32) + pair_in[0, span, :].astype(jnp.float32)
                 ).astype(jnp.bfloat16)
             if index > 0:
                 for way in range(2):
                     first_hop(part, way, index - 1).start()
         for way in range(2):
-            first_hop(part, way, ZCHUNKS - 1).start()
+            first_hop(part, way, chunks[part] - 1).start()
 
     def keep(part):
-        out_ref[part * part_rows : (part + 1) * part_rows, :] = product(part, home * 2 + core)
+        out_ref[part_span[part], :] = product(part, home * 2 + core)
 
     def pass_second(part, index):
         for way in range(2):
@@ -344,19 +342,23 @@
 
     def take(part):
         to_mate(part, 1).wait_recv()
-        for index in range(ZCHUNKS):
+        for index in range(chunks[part]):
             for way in range(2):
                 second_hop(part, way, index).wait_recv()
-                span = span_of(way, index)
-                target = pl.ds(part * part_rows + (way * ZCHUNKS + index) * chunk, chunk)
-                out_ref[target, :] = (
-                    out_ref[target, :].astype(jnp.float32)
-                    + pair_in[part, 1, span, :].astype(jnp.float32)
-                    + zin[part, span, :].astype(jnp.float32)
+                span = span_of(part, way, index)
+                out_ref[span, :] = (
+                    out_ref[span, :].astype(jnp.float32)
+                    + pair_in[1, span, :].astype(jnp.float32)
+                    + zin[span, :].astype(jnp.float32)
                 ).astype(jnp.bfloat16)
 
-    attend(0, 0, True)
-    attend(0, 1, True)
+    runs_of = [
+        [r for r in range(SUBS) if heads * part_start[p] <= r * sub < heads * (part_start[p] + part_rows[p])]
+        for p in range(PARTS)
+    ]
+    rest = [r for runs in runs_of[1:] for r in runs]
+    attend(0, runs_of[0], own=part_rows[0])
+    attend(0, rest, own=rows)
 
     kids = {}
     for edges in POINTS.values():
@@ -399,11 +401,21 @@
                 def _():
                     edge(half, origin, direction, landing).start()
 
+    def dispatch(step, whens):
+        if len(whens) == 1:
+            pl.when(step == whens[0] // 2)(functools.partial(send_on, whens[0]))
+        elif whens:
+            middle = len(whens) // 2
+            pl.when(step < whens[middle] // 2)(
+                functools.partial(dispatch, step, whens[:middle])
+            )
+            pl.when(step >= whens[middle] // 2)(
+                functools.partial(dispatch, step, whens[middle:])
+            )
+
     def visit(step, carry):
         left, unseen = carry
-        for when in sorted(POINTS):
-            if when % 2 == 0:
-                pl.when(step == when // 2)(functools.partial(send_on, when))
+        dispatch(step, [when for when in sorted(POINTS) if when % 2 == 0])
 
         @pl.when(unseen % 2 == 1)
         def _():
@@ -412,55 +424,54 @@
 
         @pl.when(left % 2 == 1)
         def _():
-            attend(step, 0, False)
-
-        for when in sorted(POINTS):
-            if when % 2 == 1:
-                pl.when(step == when // 2)(functools.partial(send_on, when))
+            attend(step, runs_of[0])
+
+        dispatch(step, [when for when in sorted(POINTS) if when % 2 == 1])
 
         @pl.when((left % 2 == 1) & (step < DEFER))
         def _():
-            attend(step, 1, False)
+            attend(step, rest)
 
         return left // 2, unseen // 2
 
     lax.fori_loop(1, len(SLOTS), visit, (wanted, late))
 
+    for slot in range(1, DEFER):
+        wanted = wanted // 2
+
+    def later(part, errands):
+        def again(step, left):
+            for when, errand in errands:
+                pl.when(step == when)(errand)
+
+            @pl.when(left % 2 == 1)
+            def _():
+                attend(step, runs_of[part])
+
+            return left // 2
+
+        lax.fori_loop(DEFER, len(SLOTS), again, wanted)
+
+    after, end = DEFER, len(SLOTS)
+    call = functools.partial
     load_o.wait()
     give(0)
-    for slot in range(1, DEFER):
-        wanted = wanted // 2
-
-    def again(step, left):
-        @pl.when(step == DEFER + 1)
-        def _():
-            pass_first(0)
-
-        for index in range(ZCHUNKS):
-            @pl.when(step == DEFER + RELAY_STEPS[index])
-            def _():
-                pass_second(0, index)
-
-        @pl.when(left % 2 == 1)
-        def _():
-            attend(step, 1, False)
-
-        return left // 2
-
-    lax.fori_loop(DEFER, len(SLOTS), again, wanted)
-    for index in range(ZCHUNKS):
-        if DEFER + RELAY_STEPS[index] >= len(SLOTS):
-            pass_second(0, index)
+    later(1, [(after + 2, call(pass_first, 0)), (end - 2, call(pass_second, 0, 0)),
+              (end - 1, call(pass_second, 0, 1))])
+    give(1)
+    later(2, [(after + 1, call(pass_second, 0, 2)), (after + 3, call(pass_first, 1)),
+              (after + 4, call(pass_second, 0, 3)), (end - 1, call(pass_second, 1, 0))])
+    give(2)
+    pass_second(1, 1)
+    pass_first(2)
     keep(0)
-
-    last = PARTS - 1
-    give(last)
-    pass_first(last)
-    keep(last)
     take(0)
-    for index in range(ZCHUNKS):
-        pass_second(last, index)
-    take(last)
+    keep(1)
+    pass_second(2, 0)
+    keep(2)
+    pass_second(2, 1)
+    take(1)
+    take(2)
 
     for origin, direction, landing in FIRST:
         @pl.when(goes(MASKS[landing], me))
@@ -478,7 +489,7 @@
     for part in range(PARTS):
         for index in range(2):
             to_mate(part, index).wait_send()
-        for index in range(ZCHUNKS):
+        for index in range(chunks[part]):
             for way in range(2):
                 first_hop(part, way, index).wait_send()
                 second_hop(part, way, index).wait_send()
@@ -515,15 +526,15 @@
             pltpu.VMEM((heads * rows, 2 * HD), bf16),
             pltpu.VMEM((heads * rows, 2 * HD), f32),
             pltpu.VMEM((heads * rows, HD), f32),
-            pltpu.VMEM((2, heads * rows // PARTS // SUBS, rows), f32),
-            pltpu.VMEM((2, heads * rows // PARTS // SUBS, rows), bf16),
-            pltpu.VMEM((2, heads * rows // PARTS // SUBS, HD), f32),
+            pltpu.VMEM((2, heads * rows // SUBS, rows), f32),
+            pltpu.VMEM((2, heads * rows // SUBS, rows), bf16),
+            pltpu.VMEM((2, heads * rows // SUBS, HD), f32),
             pltpu.VMEM((rows, heads * HD), bf16),
-            pltpu.VMEM((PARTS, 2, rows // PARTS, cols), bf16),
-            pltpu.VMEM((PARTS, 2, rows // PARTS, cols), bf16),
-            pltpu.VMEM((PARTS, rows // PARTS, cols), bf16),
-            pltpu.VMEM((PARTS, rows // PARTS, cols), bf16),
-            pltpu.VMEM((PARTS, rows // PARTS, cols), bf16),
+            pltpu.VMEM((2, rows, cols), bf16),
+            pltpu.VMEM((2, rows, cols), bf16),
+            pltpu.VMEM((rows, cols), bf16),
+            pltpu.VMEM((rows, cols), bf16),
+            pltpu.VMEM((rows, cols), bf16),
             dma((TOKEN_LOADS + 4,)),
             dma((len(SLOTS), 2)),
             dma((len(SLOTS), 2)),

time: 105 us -> 101 us (0.962)
  the two profiles are of different devices: /device:TPU:55 before, /device:TPU:57 now
where the time goes in v1:
time: 101 us; the launch traced here: 100 us
  Pallas kernels  98.2 us (97%)
  local copies, waits for them, and re-layouts  2.18 us (2%)
    pallas_call x1, Pallas kernels, body(): pl.pallas_call(kernel, out_shape=jax.ShapeDtypeStruct((rows, cols), bf16)...  98.2 us
    unnamed x1, local copies, waits for them, and re-layouts  2.18 us

profile of v1, /device:TPU:57, one launch (start us, length us, event | category | flops | bytes accessed | tf_op | source)
XLA Modules:
  0.0 100.4 jit_solution(17639187517819744439)
XLA Ops:
  0.0 98.2 %shard_map.136 = bf16[512,896]{1,0:T(8,128)(2,1)} custom-call(bf16[512,3584]{1,0:T(8,128)(2,1)} %tok_hbm.1, f32[28,128]{1,0:T(8,128)} %bitcast.6, bf16[3584,896]{1,0:T(8,128)(2,1)} %wq_hbm.1, bf16[3584,128]{1,0:T(8,128)(2,1)} %wk_hbm.1, bf16[3584,128]{1,0:T(8,128)(2,1)} %wv_hbm.1, bf16[896,3584]{1,0:T(8,128)(2,1)} %wo_hbm.1, f32[7,128]{1,0:T(8,128)} %bitcast.7, ...), custom_call_target="tpu_custom_call" | custom-call | tf_op jit(solution)/shard_map/pallas_call | solution.py:513
  98.2 2.2 %copy.16 = bf16[512,896]{1,0:T(8,128)(2,1)} copy(bf16[512,896]{1,0:T(8,128)(2,1)} %shard_map.136) | data formatting | bytes 1835008
